TPU v7x, 32 devices: a whole 2x2x4 slice. The times are simulated.
32 devices in a mesh: row: 8 (over z, x), col: 4 (over y, core).
Axes of the slice: x: 2, y: 2, z: 4, core: 2. Of those that a mesh axis runs over, the one named last changes fastest.
Arguments:
- eigvecs: bfloat16 [49152, 4096], P('row', 'col'), may hold values from -41 to 41
- reflectors: bfloat16 [8, 49152, 128], P(None, 'row'), as said below
- factors: float32 [8, 128, 128], replicated, as said below
Outputs:
- vectors: bfloat16 [49152, 4096], P('row', 'col')
- deviation: float32 [4096], P('col')
Inputs may be any that keep to these rules, and one draw needn't show every extreme that they name: `reflectors`: each panel's vectors are dense and linearly independent. factors[k] is the upper triangular compact WY factor of reflectors[k]: its inverse plus its inverse's transpose equals reflectors[k]^T reflectors[k], so that I - reflectors[k] factors[k] reflectors[k]^T is orthogonal up to rounding.
All inputs are finite; a program needn't handle non-finite values.
Results may differ from a plain program's by a relative error of at most 0.014.
Values may be sent and summed in bfloat16 or wider, within the bound.
A program may use at most 128 MiB of HBM per device.

v0:
```python
import jax
import jax.numpy as jnp
from jax import lax
from jax.sharding import PartitionSpec as P

NORD = 49152


def body(eigvecs, reflectors, factors):
    vectors = eigvecs
    panels = reflectors.shape[0]
    width = reflectors.shape[2]
    local_rows = reflectors.shape[1]
    stacked = jnp.transpose(reflectors, (1, 0, 2)).reshape(local_rows, panels * width)
    local_proj = lax.dot_general(
        stacked, eigvecs, (((0,), (0,)), ((), ())), preferred_element_type=jnp.float32
    )
    local_gram = lax.dot_general(
        stacked, stacked, (((0,), (0,)), ((), ())), preferred_element_type=jnp.float32
    )
    total_proj, total_gram = (
        lax.psum(local_proj.astype(jnp.bfloat16), "row").astype(jnp.float32),
        lax.psum(local_gram.astype(jnp.bfloat16), "row").astype(jnp.float32),
    )
    earlier = []
    for panel in range(panels):
        proj = total_proj[panel * width : (panel + 1) * width]
        for prior in range(panel):
            cross = total_gram[
                panel * width : (panel + 1) * width, prior * width : (prior + 1) * width
            ]
            proj = proj - jnp.dot(
                cross, earlier[prior].astype(jnp.float32), precision=lax.Precision.HIGHEST
            )
        scaled = jnp.dot(factors[panel], proj, precision=lax.Precision.HIGHEST).astype(jnp.bfloat16)
        earlier.append(scaled)
        update = jnp.dot(reflectors[panel], scaled, preferred_element_type=jnp.float32)
        vectors = (vectors.astype(jnp.float32) - update).astype(jnp.bfloat16)
    wide = vectors.astype(jnp.float32)
    local_squares = jnp.sum(wide * wide, axis=0)
    squares = lax.psum(local_squares, "row")
    deviation = jnp.sqrt(squares / NORD) - 1.0
    return (vectors, deviation)


def solution(mesh):
    placed = (P("row", "col"), P(None, "row", None), P())
    return jax.shard_map(
        body, mesh=mesh, in_specs=placed, out_specs=(P("row", "col"), P("col")), check_vma=False
    )
```

profile of v0, /device:TPU:0, one launch (start us, length us, event | category | flops | bytes accessed | tf_op | source)
XLA Modules:
  0.0 387.1 jit_solution(8457546555832240318)
XLA Ops:
  7.2 16.6 %copy.8 = bf16[8,6144,128]{1,2,0:T(8,128)(2,1)} copy(bf16[8,6144,128]{2,1,0:T(8,128)(2,1)} %param.4) | data formatting | bytes 25165824 | tf_op args[1]
  23.8 19.0 %convolution_convert_fusion = bf16[1024,1024]{1,0:T(8,128)(2,1)} fusion(bf16[6144,1024]{0,1:T(8,128)(2,1)} %bitcast.132), kind=kOutput, calls=%fused_computation.17 | convolution fusion | flops 12885950464 | bytes 14680064 | tf_op jit(solution)/shard_map/dot_general | solution.py:18
  42.8 16.9 %convolution_convert_fusion.1 = bf16[1024,1024]{1,0:T(8,128)(2,1)} fusion(bf16[6144,1024]{0,1:T(8,128)(2,1)} %bitcast.133, bf16[6144,1024]{1,0:T(8,128)(2,1)S(1)} %copy-done), kind=kOutput, calls=%fused_computation.18 | convolution fusion | flops 12885950464 | bytes 27262976 | tf_op jit(solution)/shard_map/dot_general | solution.py:15
  59.7 16.2 %copy.7 = bf16[6144,1024]{0,1:T(8,128)(2,1)} copy(bf16[6144,1024]{1,0:T(8,128)(2,1)} %param.3) | data formatting | bytes 25165824 | tf_op args[0]
  75.9 143.1 %all-reduce.3.cloned.1.call-done = (bf16[1024,1024]{1,0:T(8,128)(2,1)}, bf16[1024,1024]{1,0:T(8,128)(2,1)}) async-done(((bf16[1024,1024]{1,0:T(8,128)(2,1)}, bf16[1024,1024]{1,0:T(8,128)(2,1)}), (bf16[1024,1024]{1,0:T(8,128)(2,1)}, bf16[1024,1024]{1,0:T(8,128)(2,1)})) %all-reduce.3.cloned.1.call-update) | async-done | bytes 4194320 | tf_op jit(solution)/shard_map/psum | solution.py:22
  219.0 2.0 convert_element_type.126
  223.5 1.8 convolution_subtract_fusion.26
  230.2 1.8 convolution_convert_fusion.8
  232.1 9.8 %fusion.7 = bf16[6144,1024]{0,1:T(8,128)(2,1)} fusion(bf16[6144,1024]{0,1:T(8,128)(2,1)} %copy.7, bf16[1024,128]{1,0:T(8,128)(2,1)S(1)} %convolution_convert_fusion.9, bf16[8,6144,128]{2,1,0:T(8,128)(2,1)} %param.4), kind=kOutput, calls=%fused_computation.15 | convolution fusion | flops 1629487104 | bytes 27000832 | tf_op jit(solution)/shard_map/dot_general | solution.py:37
  241.9 9.8 %fusion.6 = bf16[6144,1024]{0,1:T(8,128)(2,1)} fusion(bf16[6144,1024]{0,1:T(8,128)(2,1)} %fusion.7, bf16[1024,128]{1,0:T(8,128)(2,1)S(1)} %convolution_convert_fusion.8, bf16[8,6144,128]{2,1,0:T(8,128)(2,1)} %param.4), kind=kOutput, calls=%fused_computation.13 | convolution fusion | flops 1629487104 | bytes 27000832 | tf_op jit(solution)/shard_map/dot_general | solution.py:37
  253.0 1.8 convolution_convert_fusion.7
  256.6 9.9 %fusion.5 = bf16[6144,1024]{0,1:T(8,128)(2,1)} fusion(bf16[6144,1024]{0,1:T(8,128)(2,1)} %fusion.6, bf16[1024,128]{1,0:T(8,128)(2,1)S(1)} %convolution_convert_fusion.7, bf16[8,6144,128]{2,1,0:T(8,128)(2,1)} %param.4), kind=kOutput, calls=%fused_computation.11 | convolution fusion | flops 1629487104 | bytes 27000832 | tf_op jit(solution)/shard_map/dot_general | solution.py:37
  267.4 1.8 convolution_convert_fusion.6
  271.3 9.8 %fusion.4 = bf16[6144,1024]{0,1:T(8,128)(2,1)} fusion(bf16[6144,1024]{0,1:T(8,128)(2,1)} %fusion.5, bf16[1024,128]{1,0:T(8,128)(2,1)S(1)} %convolution_convert_fusion.6, bf16[8,6144,128]{2,1,0:T(8,128)(2,1)} %param.4), kind=kOutput, calls=%fused_computation.9 | convolution fusion | flops 1629487104 | bytes 27000832 | tf_op jit(solution)/shard_map/dot_general | solution.py:37
  282.1 1.8 convolution_convert_fusion.5
  286.9 9.8 %fusion.3 = bf16[6144,1024]{0,1:T(8,128)(2,1)} fusion(bf16[6144,1024]{0,1:T(8,128)(2,1)} %fusion.4, bf16[1024,128]{1,0:T(8,128)(2,1)S(1)} %convolution_convert_fusion.5, bf16[8,6144,128]{2,1,0:T(8,128)(2,1)} %param.4), kind=kOutput, calls=%fused_computation.7 | convolution fusion | flops 1629487104 | bytes 27000832 | tf_op jit(solution)/shard_map/dot_general | solution.py:37
  297.7 1.8 convolution_convert_fusion.4
  303.5 9.8 %fusion.2 = bf16[6144,1024]{0,1:T(8,128)(2,1)} fusion(bf16[6144,1024]{0,1:T(8,128)(2,1)} %fusion.3, bf16[1024,128]{1,0:T(8,128)(2,1)S(1)} %convolution_convert_fusion.4, bf16[8,6144,128]{2,1,0:T(8,128)(2,1)} %param.4), kind=kOutput, calls=%fused_computation.5 | convolution fusion | flops 1629487104 | bytes 27000832 | tf_op jit(solution)/shard_map/dot_general | solution.py:37
  314.3 1.8 convolution_convert_fusion.3
  321.1 9.8 %fusion.1 = bf16[6144,1024]{0,1:T(8,128)(2,1)} fusion(bf16[6144,1024]{0,1:T(8,128)(2,1)} %fusion.2, bf16[1024,128]{1,0:T(8,128)(2,1)S(1)} %convolution_convert_fusion.3, bf16[8,6144,128]{2,1,0:T(8,128)(2,1)} %param.4), kind=kOutput, calls=%fused_computation.3 | convolution fusion | flops 1629487104 | bytes 27000832 | tf_op jit(solution)/shard_map/dot_general | solution.py:37
  332.0 1.8 convolution_convert_fusion.2
  333.8 10.1 %multiply_reduce_fusion = (f32[1024]{0:T(1024)S(1)}, bf16[6144,1024]{0,1:T(8,128)(2,1)}) fusion(bf16[1024,128]{1,0:T(8,128)(2,1)S(1)} %convolution_convert_fusion.2, bf16[8,6144,128]{2,1,0:T(8,128)(2,1)} %param.4, bf16[6144,1024]{0,1:T(8,128)(2,1)} %fusion.1), kind=kOutput, calls=%fused_computation.16 | convolution fusion | flops 1648360448 | bytes 27004928 | tf_op jit(solution)/shard_map/dot_general | solution.py:37
  343.9 16.6 %copy.9 = bf16[6144,1024]{1,0:T(8,128)(2,1)} copy(bf16[6144,1024]{0,1:T(8,128)(2,1)} %get-tuple-element.9) | data formatting | bytes 25165824
  360.5 19.1 %psum.23 = f32[1024]{0:T(1024)S(1)} all-reduce(f32[1024]{0:T(1024)S(1)} %get-tuple-element.8), channel_id=1, replica_groups=mesh['row'=8,'col'=4] {'row'}, use_global_device_ids=true, to_apply=%region_3.0 | all-reduce | flops 1024 | bytes 8192 | tf_op jit(solution)/shard_map/psum | solution.py:41
  (35 shorter events, 29.8 us)
Async XLA Ops:
  7.2 211.8 %all-reduce.3.cloned.1.call-start = ((), (), s32[]{:S(2)}) async-start(), calls=%async_computation | async-start | bytes 8388608 | tf_op jit(solution)/shard_map/psum | solution.py:22
  23.8 19.0 %copy-start = (bf16[6144,1024]{1,0:T(8,128)(2,1)S(1)}, bf16[6144,1024]{1,0:T(8,128)(2,1)}, u32[]{:S(2)}) copy-start(bf16[6144,1024]{1,0:T(8,128)(2,1)} %param.3) | copy-start | bytes 37748740
  256.6 9.9 %copy-start.1 = (f32[128,1024]{1,0:T(8,128)S(1)}, f32[128,1024]{1,0:T(8,128)}, u32[]{:S(2)}) copy-start(f32[128,1024]{1,0:T(8,128)} %convolution_subtract_fusion.23) | copy-start | bytes 1572868
Sparse Core Ops, SparseCore 0:
  59.9 159.1 all-reduce.2
where the time goes:
time: 391 us; the launch traced here: 387 us
  matrix products  158 us (40%)
  waiting for transfers between devices  143 us (37%)
  local copies, waits for them, and re-layouts  49.4 us (13%)
  blocking collectives  19.1 us (5%)
  between operations  14.3 us (4%)
    psum x1, waiting for transfers between devices, body(): lax.psum(local_proj.astype(jnp.bfloat16), 'row').astype(jnp.float32)  143 us
    dot_general x8, matrix products, body(): jnp.dot(reflectors[panel], scaled, preferred_element_type=jnp.float32)  78.9 us
    unnamed x7, local copies, waits for them, and re-layouts  49.4 us
    dot_general x28, matrix products, body(): jnp.dot(cross, earlier[prior].astype(jnp.float32), precision=lax.Precisio...  29.5 us
    psum x1, blocking collectives, body(): squares = lax.psum(local_squares, 'row')  19.1 us
    dot_general x1, matrix products, body(): lax.dot_general(stacked, stacked, (((0,), (0,)), ((), ())), preferred_ele...  19 us
    dot_general x1, matrix products, body(): lax.dot_general(stacked, eigvecs, (((0,), (0,)), ((), ())), preferred_ele...  16.9 us
    dot_general x8, matrix products, body(): jnp.dot(factors[panel], proj, precision=lax.Precision.HIGHEST)  14.3 us
  transfers between devices with their start and end apart: 1, of which 1 were waited for; matrix products, arithmetic and copies ran while one was open for 4% of the time, Pallas kernels for 0%

commit v1 on v0

v1 whole, which is shorter than its diff:
```python
import functools
import math

import jax
import jax.numpy as jnp
from jax import lax
from jax.experimental import pallas as pl
from jax.experimental.pallas import tpu as pltpu
from jax.sharding import PartitionSpec as P

MESH = pl.DeviceIdType.MESH
TN = (((0,), (0,)), ((), ()))
NT = (((1,), (1,)), ((), ()))


def settle(ref, sem):
    pltpu.make_async_copy(ref, ref, sem).wait()


def send(src, dst, sent, got, where):
    pltpu.make_async_remote_copy(
        src_ref=src, dst_ref=dst, send_sem=sent, recv_sem=got, device_id=where, device_id_type=MESH
    ).start()


def greet(axes):
    barrier = pltpu.get_barrier_semaphore()
    for axis, size in axes:
        me = lax.axis_index(axis)

        def hello(d, carry, axis=axis, size=size, me=me):
            pl.semaphore_signal(
                barrier, inc=1, device_id={axis: lax.rem(me + d, size)}, device_id_type=MESH
            )
            return carry

        lax.fori_loop(1, size, hello, 0)
    pl.semaphore_wait(barrier, sum(size - 1 for _, size in axes))


def scale_kernel(
    rows, cols, chunks,
    e_hbm, r_hbm, f_ref, out_hbm,
    ebuf, rbuf, acc, psend, precv, gsend, grecv, gbuf, xbuf, sbuf,
    e_sem, r_sem, p_sent, p_got, g_sent, g_got, h_sent, h_got, c_sent, c_got, s_sent, s_got, o_sem,
):
    panels, local, width = r_hbm.shape
    total = panels * width
    cw = ebuf.shape[2] // rows
    span = ebuf.shape[2]
    gs = gsend.shape[0] // rows
    depth = math.gcd(local, 1024)
    steps = local // depth
    row, col = lax.axis_index("row"), lax.axis_index("col")

    def load_r(k):
        return pltpu.make_async_copy(
            r_hbm.at[k], rbuf.at[:, pl.ds(k * width, width)], r_sem.at[k]
        )

    def load_e(j):
        return pltpu.make_async_copy(
            e_hbm.at[:, pl.ds(j * span, span)], ebuf.at[j], e_sem.at[j]
        )

    for k in range(panels):
        load_r(k).start()
    for j in range(chunks):
        load_e(j).start()
    greet((("row", rows), ("col", cols)))
    for k in range(panels):
        load_r(k).wait()

    high = panels - 1 - col

    def block(t, carry):
        flag = t // high
        panel = high + flag * (col - high)
        prior = t - flag * high

        def step(i, total_block):
            at = pl.ds(pl.multiple_of(i * depth, depth), depth)
            a = rbuf[at, pl.ds(pl.multiple_of(prior * width, width), width)]
            b = rbuf[at, pl.ds(pl.multiple_of(panel * width, width), width)]
            return total_block + lax.dot_general(a, b, TN, preferred_element_type=jnp.float32)

        result = lax.fori_loop(0, steps, step, jnp.zeros((width, width), jnp.float32))
        gsend[pl.ds(pl.multiple_of(t * width, width), width), :] = result.astype(jnp.bfloat16)
        return carry

    lax.fori_loop(0, panels, block, 0)

    def send_gram(d, carry):
        peer = lax.rem(row + d, rows)
        send(
            gsend.at[pl.ds(pl.multiple_of(peer * gs, gs), gs), :], grecv.at[d - 1],
            g_sent, g_got, {"row": peer},
        )
        return carry

    lax.fori_loop(1, rows, send_gram, 0)

    mine = pl.ds(pl.multiple_of(row * gs, gs), gs)

    def share_gram_rows():
        settle(grecv, g_got)
        part = gsend[mine, :].astype(jnp.float32)
        for d in range(rows - 1):
            part = part + grecv[d].astype(jnp.float32)
        gbuf[col, mine, :] = part.astype(jnp.bfloat16)

        def go(d, carry):
            peer = lax.rem(row + d, rows)
            send(gbuf.at[col, mine, :], gbuf.at[col, mine, :], h_sent, h_got, {"row": peer})
            return carry

        lax.fori_loop(1, rows, go, 0)

    def share_gram_cols():
        settle(gbuf.at[col, pl.ds(0, (rows - 1) * gs), :], h_got)

        def go(d, carry):
            peer = lax.rem(col + d, cols)
            send(gbuf.at[col], gbuf.at[col], c_sent, c_got, {"col": peer})
            return carry

        lax.fori_loop(1, cols, go, 0)

    for j in range(chunks):
        load_e(j).wait()
        acc[...] = jnp.zeros_like(acc)

        def step(i, carry, j=j):
            at = pl.ds(pl.multiple_of(i * depth, depth), depth)
            acc[...] += lax.dot_general(
                ebuf[j, at, :], rbuf[at, :], TN, preferred_element_type=jnp.float32
            )
            return carry

        lax.fori_loop(0, steps, step, 0)
        psend[j] = acc[...].astype(jnp.bfloat16)

        def send_proj(d, carry, j=j):
            peer = lax.rem(row + d, rows)
            send(
                psend.at[j, pl.ds(pl.multiple_of(peer * cw, cw), cw), :], precv.at[j, d - 1],
                p_sent.at[j], p_got.at[j], {"row": peer},
            )
            return carry

        lax.fori_loop(1, rows, send_proj, 0)
        if j == 0:
            share_gram_rows()
        if j == min(1, chunks - 1):
            share_gram_cols()

    own = pl.ds(pl.multiple_of(row * cw, cw), cw)
    for j in range(chunks):
        settle(precv.at[j], p_got.at[j])
        part = psend[j, own, :].astype(jnp.float32)
        for d in range(rows - 1):
            part = part + precv[j, d].astype(jnp.float32)
        xbuf[pl.ds(j * cw, cw), :] = part
    settle(gbuf.at[pl.ds(0, cols - 1)], c_got)

    done = []
    for k in range(panels):
        part = xbuf[:, k * width : (k + 1) * width]
        if k:
            place = min(k, panels - 1 - k)
            start = 0 if k >= cols else (panels - 1 - k) * width
            cross = gbuf[place, start : start + k * width, :]
            part = part - jnp.dot(
                jnp.concatenate(done, axis=1), cross, preferred_element_type=jnp.float32
            )
        part = lax.dot_general(
            part, f_ref[k], NT,
            precision=lax.Precision.HIGHEST, preferred_element_type=jnp.float32,
        ).astype(jnp.bfloat16)
        done.append(part)
        for j in range(chunks):
            sbuf[j, own, k * width : (k + 1) * width] = part[j * cw : (j + 1) * cw]

    def send_scaled(d, carry):
        peer = lax.rem(row + d, rows)
        send(sbuf.at[:, own, :], sbuf.at[:, own, :], s_sent, s_got, {"row": peer})
        return carry

    lax.fori_loop(1, rows, send_scaled, 0)
    settle(grecv, g_sent)
    settle(gbuf.at[col, pl.ds(0, (rows - 1) * gs), :], h_sent)
    settle(gbuf.at[pl.ds(0, cols - 1)], c_sent)
    for j in range(chunks):
        settle(precv.at[j], p_sent.at[j])
    rest = sbuf.at[:, pl.ds(0, (rows - 1) * cw), :]
    settle(rest, s_got)
    settle(rest, s_sent)
    result = pltpu.make_async_copy(sbuf, out_hbm, o_sem)
    result.start()
    result.wait()


def find_scaled(eigvecs, reflectors, factors, rows, cols):
    local, columns = eigvecs.shape
    panels, _, width = reflectors.shape
    total = panels * width
    chunks = max(1, min(4, columns // rows // 16, columns // 128))
    span = columns // chunks
    cw = span // rows
    gs = total // rows
    any_spec = pl.BlockSpec(memory_space=pl.ANY)
    dma = pltpu.SemaphoreType.DMA
    low = jnp.bfloat16
    scaled = pl.pallas_call(
        functools.partial(scale_kernel, rows, cols, chunks),
        out_shape=jax.ShapeDtypeStruct((chunks, span, total), low),
        in_specs=[any_spec, any_spec, pl.BlockSpec(memory_space=pltpu.VMEM)],
        out_specs=any_spec,
        scratch_shapes=[
            pltpu.VMEM((chunks, local, span), low),
            pltpu.VMEM((local, total), low),
            pltpu.VMEM((span, total), jnp.float32),
            pltpu.VMEM((chunks, span, total), low),
            pltpu.VMEM((chunks, rows - 1, cw, total), low),
            pltpu.VMEM((total, width), low),
            pltpu.VMEM((rows - 1, gs, width), low),
            pltpu.VMEM((cols, total, width), low),
            pltpu.VMEM((chunks * cw, total), jnp.float32),
            pltpu.VMEM((chunks, span, total), low),
            dma((chunks,)), dma((panels,)), dma((chunks,)), dma((chunks,)),
            dma, dma, dma, dma, dma, dma, dma, dma, dma,
        ],
        compiler_params=pltpu.CompilerParams(
            collective_id=0, has_side_effects=True, vmem_limit_bytes=60 * 1024 * 1024
        ),
    )(eigvecs, reflectors, factors)
    return scaled.reshape(columns, total)


def update_kernel(e_ref, r_ref, s_ref, v_ref, q_ref):
    panels = r_ref.shape[0]
    stacked = jnp.concatenate([r_ref[k] for k in range(panels)], axis=1)
    update = lax.dot_general(stacked, s_ref[...], NT, preferred_element_type=jnp.float32)
    vectors = (e_ref[...].astype(jnp.float32) - update).astype(jnp.bfloat16)
    v_ref[...] = vectors
    wide = vectors.astype(jnp.float32)
    squares = jnp.sum((wide * wide).reshape(-1, 8, wide.shape[1]), axis=0)

    @pl.when(pl.program_id(0) == 0)
    def _():
        q_ref[...] = jnp.zeros_like(q_ref)

    q_ref[...] += squares


def update_vectors(eigvecs, reflectors, scaled):
    local, columns = eigvecs.shape
    panels, _, width = reflectors.shape
    tile = math.gcd(local, 512)
    return pl.pallas_call(
        update_kernel,
        grid=(local // tile,),
        out_shape=(
            jax.ShapeDtypeStruct((local, columns), jnp.bfloat16),
            jax.ShapeDtypeStruct((8, columns), jnp.float32),
        ),
        in_specs=[
            pl.BlockSpec((tile, columns), lambda i: (i, 0)),
            pl.BlockSpec((panels, tile, width), lambda i: (0, i, 0)),
            pl.BlockSpec((columns, panels * width), lambda i: (0, 0)),
        ],
        out_specs=(
            pl.BlockSpec((tile, columns), lambda i: (i, 0)),
            pl.BlockSpec((8, columns), lambda i: (0, 0)),
        ),
        compiler_params=pltpu.CompilerParams(
            dimension_semantics=("arbitrary",), vmem_limit_bytes=60 * 1024 * 1024
        ),
    )(eigvecs, reflectors, scaled)


def norm_kernel(rows, q_ref, out_ref, got, sent_sem, got_sem):
    row = lax.axis_index("row")
    greet((("row", rows),))

    def go(d, carry):
        send(q_ref, got.at[d - 1], sent_sem, got_sem, {"row": lax.rem(row + d, rows)})
        return carry

    lax.fori_loop(1, rows, go, 0)
    settle(got, got_sem)
    part = q_ref[...]
    for d in range(rows - 1):
        part = part + got[d]
    out_ref[...] = part
    settle(got, sent_sem)


def sum_squares(squares, rows):
    vmem = pl.BlockSpec(memory_space=pltpu.VMEM)
    return pl.pallas_call(
        functools.partial(norm_kernel, rows),
        out_shape=jax.ShapeDtypeStruct(squares.shape, squares.dtype),
        in_specs=[vmem],
        out_specs=vmem,
        scratch_shapes=[
            pltpu.VMEM((rows - 1,) + squares.shape, squares.dtype),
            pltpu.SemaphoreType.DMA,
            pltpu.SemaphoreType.DMA,
        ],
        compiler_params=pltpu.CompilerParams(collective_id=1, has_side_effects=True),
    )(squares)


def body(eigvecs, reflectors, factors, order, rows, cols):
    scaled = find_scaled(eigvecs, reflectors, factors, rows, cols)
    vectors, squares = update_vectors(eigvecs, reflectors, scaled)
    columns = eigvecs.shape[1]
    squares = sum_squares(jnp.sum(squares, axis=0).reshape(8, columns // 8), rows)
    return (vectors, jnp.sqrt(squares.reshape(columns) / order) - 1.0)


def solution(mesh):
    placed = (P("row", "col"), P(None, "row", None), P())
    rows, cols = mesh.shape["row"], mesh.shape["col"]

    def whole(eigvecs, reflectors, factors):
        order = eigvecs.shape[0]
        return jax.shard_map(
            lambda e, r, f: body(e, r, f, order, rows, cols),
            mesh=mesh,
            in_specs=placed,
            out_specs=(P("row", "col"), P("col")),
            check_vma=False,
        )(eigvecs, reflectors, factors)

    return whole
```

time: 391 us -> 169 us (0.43)
  Pallas kernels: 0 us -> 165 us
  matrix products: 158 us -> 0 us
  waiting for transfers between devices: 143 us -> 0 us
  local copies, waits for them, and re-layouts: 49.4 us -> 0 us
  blocking collectives: 19.1 us -> 0 us
  between operations: 14.3 us -> 0.65 us
    pallas_call x0 -> x3, Pallas kernels: none -> 165 us  [the longest x1 119 us: find_scaled(): pl.pallas_call(functools.partial(scale_kernel, rows, cols, chunks), out_s...]
    dot_general x46 -> x0, matrix products: 158 us -> none  [the longest x8 78.9 us: body(): jnp.dot(reflectors[panel], scaled, preferred_element_type=jnp.float32)]
    psum x1 -> x0, waiting for transfers between devices: 143 us -> none  [body(): lax.psum(local_proj.astype(jnp.bfloat16), 'row').astype(jnp.float32)]
    unnamed x7 -> x0, local copies, waits for them, and re-layouts: 49.4 us -> none
    psum x1 -> x0, blocking collectives: 19.1 us -> none  [body(): squares = lax.psum(local_squares, 'row')]
  transfers between devices with their start and end apart: 1 -> 0, of which waited for: 1 -> 0; matrix products, arithmetic and copies ran while one was open for 4% -> 0% of each run, Pallas kernels for 0% -> 0%
where the time goes in v1:
time: 169 us; the launch traced here: 168 us
  Pallas kernels  165 us (98%)
  other arithmetic  2.64 us (2%)
    pallas_call x1, Pallas kernels, find_scaled(): pl.pallas_call(functools.partial(scale_kernel, rows, cols, chunks), out_s...  119 us
    pallas_call x1, Pallas kernels, update_vectors(): pl.pallas_call(update_kernel, grid=(local // tile,), out_shape=(jax.Shape...  23.4 us
    pallas_call x1, Pallas kernels, sum_squares(): pl.pallas_call(functools.partial(norm_kernel, rows), out_shape=jax.ShapeD...  22.3 us

profile of v1, /device:TPU:0, one launch (start us, length us, event | category | flops | bytes accessed | tf_op | source)
XLA Modules:
  0.0 168.0 jit_solution(12205891680518753394)
XLA Ops:
  0.6 119.0 %shard_map.50 = bf16[4,256,1024]{2,1,0:T(8,128)(2,1)} custom-call(bf16[6144,1024]{1,0:T(8,128)(2,1)} %e_ref.1, bf16[8,6144,128]{2,1,0:T(8,128)(2,1)} %r_ref.1, f32[8,128,128]{2,1,0:T(8,128)} %f_ref.1), custom_call_target="tpu_custom_call" | custom-call | tf_op jit(solution)/shard_map/pallas_call | solution.py:214
  119.7 23.4 %shard_map.51 = (bf16[6144,1024]{1,0:T(8,128)(2,1)}, f32[8,1024]{1,0:T(8,128)}) custom-call(bf16[6144,1024]{1,0:T(8,128)(2,1)} %e_ref.1, bf16[8,6144,128]{2,1,0:T(8,128)(2,1)} %r_ref.1, bf16[1024,1024]{1,0:T(8,128)(2,1)} %bitcast.4), custom_call_target="tpu_custom_call" | custom-call | tf_op jit(solution)/shard_map/pallas_call | solution.py:260
  143.1 1.4 reduce_sum.9
  144.5 22.3 %shard_map.52 = f32[8,128]{1,0:T(8,128)} custom-call(f32[8,128]{1,0:T(8,128)} %bitcast.5), custom_call_target="tpu_custom_call" | custom-call | tf_op jit(solution)/shard_map/pallas_call | solution.py:301
  166.7 1.3 add_bitcast_fusion

commit v2 on v1

--- a/solution.py
+++ b/solution.py
@@ -41,8 +41,8 @@
 def scale_kernel(
     rows, cols, chunks,
     e_hbm, r_hbm, f_ref, out_hbm,
-    ebuf, rbuf, acc, psend, precv, gsend, grecv, gbuf, xbuf, sbuf,
-    e_sem, r_sem, p_sent, p_got, g_sent, g_got, h_sent, h_got, c_sent, c_got, s_sent, s_got, o_sem,
+    ebuf, rbuf, acc, psend, xrecv, mid, precv, gsend, grecv, gbuf, xbuf, sbuf,
+    e_sem, r_sem, p_sent, p_got, g_sent, g_got, h_sent, h_got, c_sent, c_got, s_sent, s_got, m_sent, m_got, x_sent, x_got, o_sem,
 ):
     panels, local, width = r_hbm.shape
     total = panels * width
@@ -52,6 +52,10 @@
     depth = math.gcd(local, 1024)
     steps = local // depth
     row, col = lax.axis_index("row"), lax.axis_index("col")
+    outer, half = rows // 2, span // 2
+    place, side = row // 2, row % 2
+    partner = {"row": row + 1 - 2 * side}
+    own = pl.ds(pl.multiple_of(side * half + place * cw, cw), cw)
 
     def load_r(k):
         return pltpu.make_async_copy(
@@ -88,8 +92,6 @@
         gsend[pl.ds(pl.multiple_of(t * width, width), width), :] = result.astype(jnp.bfloat16)
         return carry
 
-    lax.fori_loop(0, panels, block, 0)
-
     def send_gram(d, carry):
         peer = lax.rem(row + d, rows)
         send(
@@ -98,8 +100,6 @@
         )
         return carry
 
-    lax.fori_loop(1, rows, send_gram, 0)
-
     mine = pl.ds(pl.multiple_of(row * gs, gs), gs)
 
     def share_gram_rows():
@@ -126,6 +126,22 @@
 
         lax.fori_loop(1, cols, go, 0)
 
+    def pass_on(j):
+        settle(xrecv.at[j], p_got.at[j])
+        kept = pl.ds(pl.multiple_of(side * half, half), half)
+        both = psend[j, kept, :].astype(jnp.float32) + xrecv[j].astype(jnp.float32)
+        mid[j] = both.astype(jnp.bfloat16)
+
+        def go(d, carry):
+            peer = lax.rem(place + d, outer)
+            send(
+                mid.at[j, pl.ds(pl.multiple_of(peer * cw, cw), cw), :], precv.at[j, d - 1],
+                m_sent.at[j], m_got.at[j], {"row": 2 * peer + side},
+            )
+            return carry
+
+        lax.fori_loop(1, outer, go, 0)
+
     for j in range(chunks):
         load_e(j).wait()
         acc[...] = jnp.zeros_like(acc)
@@ -140,25 +156,23 @@
         lax.fori_loop(0, steps, step, 0)
         psend[j] = acc[...].astype(jnp.bfloat16)
 
-        def send_proj(d, carry, j=j):
-            peer = lax.rem(row + d, rows)
-            send(
-                psend.at[j, pl.ds(pl.multiple_of(peer * cw, cw), cw), :], precv.at[j, d - 1],
-                p_sent.at[j], p_got.at[j], {"row": peer},
-            )
-            return carry
-
-        lax.fori_loop(1, rows, send_proj, 0)
+        other = pl.ds(pl.multiple_of((1 - side) * half, half), half)
+        send(psend.at[j, other, :], xrecv.at[j], p_sent.at[j], p_got.at[j], partner)
         if j == 0:
+            lax.fori_loop(0, panels, block, 0)
+            lax.fori_loop(1, rows, send_gram, 0)
+        if j:
+            pass_on(j - 1)
+        if j == min(1, chunks - 1):
             share_gram_rows()
-        if j == min(1, chunks - 1):
+        if j == min(2, chunks - 1):
             share_gram_cols()
 
-    own = pl.ds(pl.multiple_of(row * cw, cw), cw)
+    pass_on(chunks - 1)
     for j in range(chunks):
-        settle(precv.at[j], p_got.at[j])
-        part = psend[j, own, :].astype(jnp.float32)
-        for d in range(rows - 1):
+        settle(precv.at[j], m_got.at[j])
+        part = mid[j, pl.ds(pl.multiple_of(place * cw, cw), cw), :].astype(jnp.float32)
+        for d in range(outer - 1):
             part = part + precv[j, d].astype(jnp.float32)
         xbuf[pl.ds(j * cw, cw), :] = part
     settle(gbuf.at[pl.ds(0, cols - 1)], c_got)
@@ -167,9 +181,9 @@
     for k in range(panels):
         part = xbuf[:, k * width : (k + 1) * width]
         if k:
-            place = min(k, panels - 1 - k)
+            slot = min(k, panels - 1 - k)
             start = 0 if k >= cols else (panels - 1 - k) * width
-            cross = gbuf[place, start : start + k * width, :]
+            cross = gbuf[slot, start : start + k * width, :]
             part = part - jnp.dot(
                 jnp.concatenate(done, axis=1), cross, preferred_element_type=jnp.float32
             )
@@ -181,20 +195,34 @@
         for j in range(chunks):
             sbuf[j, own, k * width : (k + 1) * width] = part[j * cw : (j + 1) * cw]
 
+    send(sbuf.at[:, own, :], sbuf.at[:, own, :], x_sent, x_got, partner)
+
     def send_scaled(d, carry):
-        peer = lax.rem(row + d, rows)
-        send(sbuf.at[:, own, :], sbuf.at[:, own, :], s_sent, s_got, {"row": peer})
-        return carry
-
-    lax.fori_loop(1, rows, send_scaled, 0)
+        peer = 2 * lax.rem(place + d, outer) + side
+        send(
+            sbuf.at[:, own, :], sbuf.at[:, own, :], s_sent, s_got.at[d - 1], {"row": peer}
+        )
+        return carry
+
+    lax.fori_loop(1, outer, send_scaled, 0)
+
+    def forward(d, carry):
+        source = lax.rem(place + outer - d, outer)
+        block = sbuf.at[:, pl.ds(pl.multiple_of(side * half + source * cw, cw), cw), :]
+        settle(block, s_got.at[d - 1])
+        send(block, block, x_sent, x_got, partner)
+        return carry
+
+    lax.fori_loop(1, outer, forward, 0)
     settle(grecv, g_sent)
     settle(gbuf.at[col, pl.ds(0, (rows - 1) * gs), :], h_sent)
     settle(gbuf.at[pl.ds(0, cols - 1)], c_sent)
     for j in range(chunks):
-        settle(precv.at[j], p_sent.at[j])
-    rest = sbuf.at[:, pl.ds(0, (rows - 1) * cw), :]
-    settle(rest, s_got)
-    settle(rest, s_sent)
+        settle(xrecv.at[j], p_sent.at[j])
+        settle(precv.at[j], m_sent.at[j])
+    settle(sbuf.at[:, pl.ds(0, (outer - 1) * cw), :], s_sent)
+    settle(sbuf.at[:, pl.ds(0, half), :], x_got)
+    settle(sbuf.at[:, pl.ds(0, half), :], x_sent)
     result = pltpu.make_async_copy(sbuf, out_hbm, o_sem)
     result.start()
     result.wait()
@@ -221,14 +249,17 @@
             pltpu.VMEM((local, total), low),
             pltpu.VMEM((span, total), jnp.float32),
             pltpu.VMEM((chunks, span, total), low),
-            pltpu.VMEM((chunks, rows - 1, cw, total), low),
+            pltpu.VMEM((chunks, span // 2, total), low),
+            pltpu.VMEM((chunks, span // 2, total), low),
+            pltpu.VMEM((chunks, rows // 2 - 1, cw, total), low),
             pltpu.VMEM((total, width), low),
             pltpu.VMEM((rows - 1, gs, width), low),
             pltpu.VMEM((cols, total, width), low),
             pltpu.VMEM((chunks * cw, total), jnp.float32),
             pltpu.VMEM((chunks, span, total), low),
             dma((chunks,)), dma((panels,)), dma((chunks,)), dma((chunks,)),
-            dma, dma, dma, dma, dma, dma, dma, dma, dma,
+            dma, dma, dma, dma, dma, dma, dma, dma((rows // 2 - 1,)),
+            dma((chunks,)), dma((chunks,)), dma, dma, dma,
         ],
         compiler_params=pltpu.CompilerParams(
             collective_id=0, has_side_effects=True, vmem_limit_bytes=60 * 1024 * 1024

time: 169 us -> 140 us (0.83)
  Pallas kernels: 165 us -> 136 us
    pallas_call x1, Pallas kernels: 119 us -> 101 us  [find_scaled(): pl.pallas_call(functools.partial(scale_kernel, rows, cols, chunks), out_s...]
    pallas_call x1, Pallas kernels: 22.3 us -> 11.6 us  [sum_squares(): pl.pallas_call(functools.partial(norm_kernel, rows), out_shape=jax.ShapeD...]
where the time goes in v2:
time: 140 us; the launch traced here: 139 us
  Pallas kernels  136 us (97%)
  other arithmetic  2.64 us (2%)
    pallas_call x1, Pallas kernels, find_scaled(): pl.pallas_call(functools.partial(scale_kernel, rows, cols, chunks), out_s...  101 us
    pallas_call x1, Pallas kernels, update_vectors(): pl.pallas_call(update_kernel, grid=(local // tile,), out_shape=(jax.Shape...  23.4 us
    pallas_call x1, Pallas kernels, sum_squares(): pl.pallas_call(functools.partial(norm_kernel, rows), out_shape=jax.ShapeD...  11.6 us

profile of v2, /device:TPU:0, one launch (start us, length us, event | category | flops | bytes accessed | tf_op | source)
XLA Modules:
  0.0 138.9 jit_solution(7841153808079021496)
XLA Ops:
  0.6 100.6 %shard_map.50 = bf16[4,256,1024]{2,1,0:T(8,128)(2,1)} custom-call(bf16[6144,1024]{1,0:T(8,128)(2,1)} %e_ref.1, bf16[8,6144,128]{2,1,0:T(8,128)(2,1)} %r_ref.1, f32[8,128,128]{2,1,0:T(8,128)} %f_ref.1), custom_call_target="tpu_custom_call" | custom-call | tf_op jit(solution)/shard_map/pallas_call | solution.py:242
  101.2 23.4 %shard_map.51 = (bf16[6144,1024]{1,0:T(8,128)(2,1)}, f32[8,1024]{1,0:T(8,128)}) custom-call(bf16[6144,1024]{1,0:T(8,128)(2,1)} %e_ref.1, bf16[8,6144,128]{2,1,0:T(8,128)(2,1)} %r_ref.1, bf16[1024,1024]{1,0:T(8,128)(2,1)} %bitcast.4), custom_call_target="tpu_custom_call" | custom-call | tf_op jit(solution)/shard_map/pallas_call | solution.py:291
  124.6 1.4 reduce_sum.9
  126.0 11.6 %shard_map.52 = f32[8,128]{1,0:T(8,128)} custom-call(f32[8,128]{1,0:T(8,128)} %bitcast.5), custom_call_target="tpu_custom_call" | custom-call | tf_op jit(solution)/shard_map/pallas_call | solution.py:332
  137.7 1.3 add_bitcast_fusion
